TPU v7x, 32 devices: a whole 2x2x4 slice. The times are simulated.
32 devices in a mesh: expert: 4 (over y, core), shard: 8 (over z, x).
Axes of the slice: x: 2, y: 2, z: 4, core: 2. Of those that a mesh axis runs over, the one named last changes fastest.
Arguments:
- master_down: float32 [16, 6400, 4096], P('expert', None, 'shard'), may hold values from -0.109375 to 0.109375
- second_down: bfloat16 [16, 6400, 4096], P('expert', None, 'shard'), may hold values from -0.0390625 to 0.0390625
- router_weight: float32 [4096, 16], P('shard', 'expert'), may hold values from -0.09375 to 0.09375
- router_gain: float32 [4096], P('shard'), may hold values from 0.25 to 1.75
Outputs:
- final_down: bfloat16 [16, 6400, 4096], P('expert', 'shard')
- scale_down: float32 [16, 6400], P('expert', 'shard')
- serve_router: bfloat16 [4096, 16], replicated
All inputs are finite; a program needn't handle non-finite values.
Results may differ from a plain program's by a relative error of at most 0.0085.
Values may be sent and summed in bfloat16 or wider, within the bound.
A program may use at most 256 MiB of HBM per device.

v0:
```python
import jax
import jax.numpy as jnp
from jax import lax
from jax.sharding import PartitionSpec as P


def body(master_down, second_down, router_weight, router_gain):
    merged_down = master_down + second_down.astype(jnp.float32)
    total_down = lax.psum(
        jnp.sum(merged_down * merged_down, axis=2).astype(jnp.bfloat16), "shard"
    ).astype(jnp.float32)
    scale_down = jnp.sqrt(total_down)
    narrow_down = (merged_down / jnp.expand_dims(scale_down, 2)).astype(jnp.bfloat16)
    final_down = lax.all_to_all(narrow_down, "shard", split_axis=1, concat_axis=2, tiled=True)
    scale_down = lax.dynamic_slice_in_dim(
        scale_down, lax.axis_index("shard") * final_down.shape[1], final_down.shape[1], axis=1
    )
    part_router = (router_weight * router_gain[:, None]).astype(jnp.bfloat16)
    row_router = lax.all_gather(part_router, "shard", axis=0, tiled=True)
    serve_router = lax.all_gather(row_router, "expert", axis=1, tiled=True)
    return (final_down, scale_down, serve_router)


def solution(mesh):
    placed = (
        P("expert", None, "shard"),
        P("expert", None, "shard"),
        P("shard", "expert"),
        P("shard"),
    )
    return jax.shard_map(
        body,
        mesh=mesh,
        in_specs=placed,
        out_specs=(P("expert", "shard", None), P("expert", "shard"), P()),
        check_vma=False,
    )
```

profile of v0, /device:TPU:0, one launch (start us, length us, event | category | flops | bytes accessed | tf_op | source)
XLA Modules:
  0.0 826.9 jit_solution(7862156734528137198)
XLA Ops:
  0.6 24.2 %multiply_reduce_fusion = bf16[4,6400]{1,0:T(4,128)(2,1)S(1)} fusion(f32[4,6400,512]{2,1,0:T(8,128)} %param.4, bf16[4,6400,512]{2,1,0:T(8,128)(2,1)} %param.5), kind=kLoop, calls=%fused_computation.1 | loop fusion | flops 52403200 | bytes 78694400 | tf_op jit(solution)/shard_map/reduce_sum | solution.py:10
  24.9 0.9 copy.21
  25.8 83.5 %psum.7 = bf16[4,6400]{0,1:T(8,128)(2,1)} all-reduce(bf16[4,6400]{0,1:T(8,128)(2,1)S(1)} %copy.21), channel_id=1, replica_groups=mesh['expert'=4,'shard'=8] {'shard'}, use_global_device_ids=true, to_apply=%region_1.0 | all-reduce | flops 25600 | bytes 102400 | tf_op jit(solution)/shard_map/psum | solution.py:9
  109.3 2.3 convert_sqrt_fusion
  111.6 1.2 copy.17
  112.8 34.3 %divide_convert_fusion = bf16[4,6400,512]{2,1,0:T(8,128)(2,1)} fusion(f32[4,6400,512]{2,1,0:T(8,128)} %param.4, bf16[4,6400,512]{2,1,0:T(8,128)(2,1)} %param.5, f32[4,6400]{1,0:T(4,128)S(1)} %copy.17), kind=kLoop, calls=%fused_computation | loop fusion | flops 52428800 | bytes 104960000 | tf_op jit(solution)/shard_map/convert_element_type | solution.py:13
  147.1 33.4 %copy.18 = bf16[4,6400,512]{2,0,1:T(4,128)(2,1)} copy(bf16[4,6400,512]{2,1,0:T(8,128)(2,1)} %divide_convert_fusion) | data formatting | bytes 52428800 | tf_op jit(solution)/shard_map/convert_element_type | solution.py:13
  180.5 0.0 copy-start
  180.5 0.0 copy-start.1
  180.5 6.6 all-to-all-start
  187.2 0.8 constant_dynamic-slice_fusion
  187.9 1.8 copy.20
  189.7 0.0 copy-done
  189.7 0.0 copy-done.1
  189.7 573.7 %all_gather.6 = bf16[4096,4]{0,1:T(4,128)(2,1)S(1)} all-gather(bf16[512,4]{0,1:T(4,128)(2,1)S(1)} %multiply_convert_fusion), channel_id=1, replica_groups=mesh['expert'=4,'shard'=8] {'shard'}, dimensions={0}, use_global_device_ids=true | all-gather | bytes 36864 | tf_op jit(solution)/shard_map/all_gather | solution.py:19
  763.4 5.4 all-gather
  768.8 0.7 reshape.9
  769.5 0.0 all-to-all-done
  769.5 18.2 %copy.19 = bf16[4,800,8,512]{3,2,1,0:T(8,128)(2,1)} copy(bf16[4,800,8,512]{3,0,1,2:T(4,128)(2,1)} %bitcast.1) | data formatting | bytes 52428800 | tf_op jit(solution)/shard_map/all_to_all | solution.py:14
  787.7 39.2 %all_to_all.16 = bf16[4,800,4096]{2,1,0:T(8,128)(2,1)} reshape(bf16[4,800,8,512]{3,2,1,0:T(8,128)(2,1)} %copy.19) | data formatting | bytes 52428800 | tf_op jit(solution)/shard_map/all_to_all | solution.py:14
  (1 shorter events, 0.0 us)
Async XLA Ops:
  180.5 9.2 %copy-start = (f32[512,4]{0,1:T(4,128)S(1)}, f32[512,4]{0,1:T(4,128)}, u32[]{:S(2)}) copy-start(f32[512,4]{0,1:T(4,128)} %param.6) | copy-start | bytes 24580
  180.5 9.2 %copy-start.1 = (f32[512]{0:T(512)S(1)}, f32[512]{0:T(512)}, u32[]{:S(2)}) copy-start(f32[512]{0:T(512)} %param.7) | copy-start | bytes 6148
  180.5 589.0 %all-to-all-start = ((bf16[4,6400,512]{2,0,1:T(4,128)(2,1)}), bf16[4,6400,512]{2,0,1:T(4,128)(2,1)}, u32[]{:S(2)}, u32[]{:S(2)}) async-start(bf16[4,6400,512]{2,0,1:T(4,128)(2,1)} %copy.18), calls=%async_computation | async-start | bytes 52428800 | tf_op jit(solution)/shard_map/all_to_all | solution.py:14
where the time goes:
time: 828 us; the launch traced here: 827 us
  blocking collectives  663 us (80%)
  local copies, waits for them, and re-layouts  96.2 us (12%)
  other arithmetic  60.8 us (7%)
    all_gather x1, blocking collectives, body(): row_router = lax.all_gather(part_router, 'shard', axis=0, tiled=True)  574 us
    psum x1, blocking collectives, body(): lax.psum(jnp.sum(merged_down * merged_down, axis=2).astype(jnp.bfloat16),...  83.5 us
    all_to_all x2, local copies, waits for them, and re-layouts, body(): lax.all_to_all(narrow_down, 'shard', split_axis=1, concat_axis=2, tiled=T...  57.4 us
    convert_element_type x1, other arithmetic, body(): (merged_down / jnp.expand_dims(scale_down, 2)).astype(jnp.bfloat16)  34.3 us
    convert_element_type x1, local copies, waits for them, and re-layouts, body(): (merged_down / jnp.expand_dims(scale_down, 2)).astype(jnp.bfloat16)  33.4 us
    reduce_sum x1, other arithmetic, body(): jnp.sum(merged_down * merged_down, axis=2).astype(jnp.bfloat16)  24.2 us
  transfers between devices with their start and end apart: 1, of which 0 were waited for; matrix products, arithmetic and copies ran while one was open for 0% of the time, Pallas kernels for 0%

commit v1 on v0

--- a/solution.py
+++ b/solution.py
@@ -6,8 +6,9 @@
 
 def body(master_down, second_down, router_weight, router_gain):
     merged_down = master_down + second_down.astype(jnp.float32)
-    total_down = lax.psum(
-        jnp.sum(merged_down * merged_down, axis=2).astype(jnp.bfloat16), "shard"
+    total_down = jnp.sum(
+        lax.all_gather(jnp.sum(merged_down * merged_down, axis=2).astype(jnp.bfloat16), "shard"),
+        axis=0,
     ).astype(jnp.float32)
     scale_down = jnp.sqrt(total_down)
     narrow_down = (merged_down / jnp.expand_dims(scale_down, 2)).astype(jnp.bfloat16)

time: 828 us -> 779 us (0.941)
  blocking collectives: 663 us -> 618 us
    psum x1 -> x0, blocking collectives: 83.5 us -> none  [body(): lax.psum(jnp.sum(merged_down * merged_down, axis=2).astype(jnp.bfloat16),...]
    all_gather x0 -> x1, blocking collectives: none -> 32.8 us  [body(): lax.all_gather(jnp.sum(merged_down * merged_down, axis=2).astype(jnp.bflo...]
where the time goes in v1:
time: 779 us; the launch traced here: 777 us
  blocking collectives  618 us (79%)
  local copies, waits for them, and re-layouts  93.8 us (12%)
  other arithmetic  58.8 us (8%)
    all_gather x1, blocking collectives, body(): row_router = lax.all_gather(part_router, 'shard', axis=0, tiled=True)  579 us
    all_to_all x2, local copies, waits for them, and re-layouts, body(): lax.all_to_all(narrow_down, 'shard', split_axis=1, concat_axis=2, tiled=T...  57.4 us
    convert_element_type x1, other arithmetic, body(): (merged_down / jnp.expand_dims(scale_down, 2)).astype(jnp.bfloat16)  34.3 us
    convert_element_type x1, local copies, waits for them, and re-layouts, body(): (merged_down / jnp.expand_dims(scale_down, 2)).astype(jnp.bfloat16)  33.4 us
    all_gather x1, blocking collectives, body(): lax.all_gather(jnp.sum(merged_down * merged_down, axis=2).astype(jnp.bflo...  32.8 us
    reduce_sum x1, other arithmetic, body(): jnp.sum(merged_down * merged_down, axis=2).astype(jnp.bfloat16)  24.2 us
  transfers between devices with their start and end apart: 1, of which 0 were waited for; matrix products, arithmetic and copies ran while one was open for 0% of the time, Pallas kernels for 0%

profile of v1, /device:TPU:0, one launch (start us, length us, event | category | flops | bytes accessed | tf_op | source)
XLA Modules:
  0.0 777.5 jit_solution(17265991484088323087)
XLA Ops:
  0.6 24.2 %multiply_reduce_fusion = bf16[4,6400]{1,0:T(4,128)(2,1)S(1)} fusion(f32[4,6400,512]{2,1,0:T(8,128)} %param.4, bf16[4,6400,512]{2,1,0:T(8,128)(2,1)} %param.5), kind=kLoop, calls=%fused_computation.1 | loop fusion | flops 52403200 | bytes 78694400 | tf_op jit(solution)/shard_map/reduce_sum | solution.py:10
  24.9 0.9 copy.21
  25.8 0.8 copy.18
  26.6 32.8 %all-gather.1 = bf16[8,4,6400]{2,1,0:T(4,128)(2,1)S(1)} all-gather(bf16[1,4,6400]{2,1,0:T(4,128)(2,1)S(1)} %copy.18), channel_id=2, replica_groups=mesh['expert'=4,'shard'=8] {'shard'}, dimensions={0}, use_global_device_ids=true | all-gather | bytes 460800 | tf_op jit(solution)/shard_map/all_gather | solution.py:10
  59.4 0.2 reduce_sum.22
  59.6 0.1 convert_sqrt_fusion
  59.6 34.3 %divide_convert_fusion = bf16[4,6400,512]{2,1,0:T(8,128)(2,1)} fusion(f32[4,6400,512]{2,1,0:T(8,128)} %param.4, bf16[4,6400,512]{2,1,0:T(8,128)(2,1)} %param.5, f32[4,6400]{1,0:T(4,128)S(1)} %convert_sqrt_fusion), kind=kLoop, calls=%fused_computation | loop fusion | flops 52428800 | bytes 104960000 | tf_op jit(solution)/shard_map/convert_element_type | solution.py:14
  93.9 0.0 copy-start
  93.9 0.0 copy-start.1
  93.9 33.4 %copy.19 = bf16[4,6400,512]{2,0,1:T(4,128)(2,1)} copy(bf16[4,6400,512]{2,1,0:T(8,128)(2,1)} %divide_convert_fusion) | data formatting | bytes 52428800 | tf_op jit(solution)/shard_map/convert_element_type | solution.py:14
  127.3 6.5 all-to-all-start
  133.8 0.0 copy-done
  133.8 0.0 copy-done.1
  133.9 579.4 %all_gather.11 = bf16[4096,4]{0,1:T(4,128)(2,1)S(1)} all-gather(bf16[512,4]{0,1:T(4,128)(2,1)S(1)} %multiply_convert_fusion), channel_id=1, replica_groups=mesh['expert'=4,'shard'=8] {'shard'}, dimensions={0}, use_global_device_ids=true | all-gather | bytes 36864 | tf_op jit(solution)/shard_map/all_gather | solution.py:20
  713.3 5.4 all-gather.2
  718.7 0.7 reshape.23
  719.4 0.7 constant_dynamic-slice_fusion
  720.1 0.0 all-to-all-done
  720.1 18.2 %copy.20 = bf16[4,800,8,512]{3,2,1,0:T(8,128)(2,1)} copy(bf16[4,800,8,512]{3,0,1,2:T(4,128)(2,1)} %bitcast.2) | data formatting | bytes 52428800 | tf_op jit(solution)/shard_map/all_to_all | solution.py:15
  738.3 39.2 %all_to_all.16 = bf16[4,800,4096]{2,1,0:T(8,128)(2,1)} reshape(bf16[4,800,8,512]{3,2,1,0:T(8,128)(2,1)} %copy.20) | data formatting | bytes 52428800 | tf_op jit(solution)/shard_map/all_to_all | solution.py:15
  (1 shorter events, 0.0 us)
Async XLA Ops:
  93.9 39.9 %copy-start = (f32[512,4]{0,1:T(4,128)S(1)}, f32[512,4]{0,1:T(4,128)}, u32[]{:S(2)}) copy-start(f32[512,4]{0,1:T(4,128)} %param.6) | copy-start | bytes 24580
  93.9 39.9 %copy-start.1 = (f32[512]{0:T(512)S(1)}, f32[512]{0:T(512)}, u32[]{:S(2)}) copy-start(f32[512]{0:T(512)} %param.7) | copy-start | bytes 6148
  127.3 592.7 %all-to-all-start = ((bf16[4,6400,512]{2,0,1:T(4,128)(2,1)}), bf16[4,6400,512]{2,0,1:T(4,128)(2,1)}, u32[]{:S(2)}, u32[]{:S(2)}) async-start(bf16[4,6400,512]{2,0,1:T(4,128)(2,1)} %copy.19), calls=%async_computation | async-start | bytes 52428800 | tf_op jit(solution)/shard_map/all_to_all | solution.py:15

commit v2 on v0

--- a/solution.py
+++ b/solution.py
@@ -11,7 +11,12 @@
     ).astype(jnp.float32)
     scale_down = jnp.sqrt(total_down)
     narrow_down = (merged_down / jnp.expand_dims(scale_down, 2)).astype(jnp.bfloat16)
-    final_down = lax.all_to_all(narrow_down, "shard", split_axis=1, concat_axis=2, tiled=True)
+    final_down = jnp.concatenate(
+        lax.all_to_all(
+            jnp.stack(jnp.split(narrow_down, lax.axis_size("shard"), axis=1)), "shard", 0, 0
+        ),
+        axis=2,
+    )
     scale_down = lax.dynamic_slice_in_dim(
         scale_down, lax.axis_index("shard") * final_down.shape[1], final_down.shape[1], axis=1
     )

time: 828 us -> 739 us (0.89)
  local copies, waits for them, and re-layouts: 96.2 us -> 49.8 us
  blocking collectives: 663 us -> 623 us
    all_to_all x2 -> x0, local copies, waits for them, and re-layouts: 57.4 us -> none  [body(): lax.all_to_all(narrow_down, 'shard', split_axis=1, concat_axis=2, tiled=T...]
    psum x1, blocking collectives: 83.5 us -> 39.3 us  [body(): lax.psum(jnp.sum(merged_down * merged_down, axis=2).astype(jnp.bfloat16),...]
    convert_element_type x1 -> x0, local copies, waits for them, and re-layouts: 33.4 us -> none  [body(): (merged_down / jnp.expand_dims(scale_down, 2)).astype(jnp.bfloat16)]
    unnamed x7 -> x12, local copies, waits for them, and re-layouts: 3.4 us -> 27.5 us
    reshape x0 -> x1, local copies, waits for them, and re-layouts: none -> 17.9 us  [body(): jnp.concatenate(lax.all_to_all(jnp.stack(jnp.split(narrow_down, lax.axis_...]
where the time goes in v2:
time: 739 us
  blocking collectives  623 us (84%)
  other arithmetic  58.6 us (8%)
  local copies, waits for them, and re-layouts  49.8 us (7%)
    all_gather x1, blocking collectives, body(): row_router = lax.all_gather(part_router, 'shard', axis=0, tiled=True)  578 us
    psum x1, blocking collectives, body(): lax.psum(jnp.sum(merged_down * merged_down, axis=2).astype(jnp.bfloat16),...  39.3 us
    convert_element_type x1, other arithmetic, body(): (merged_down / jnp.expand_dims(scale_down, 2)).astype(jnp.bfloat16)  34.3 us
    unnamed x12, local copies, waits for them, and re-layouts  27.5 us
    reduce_sum x1, other arithmetic, body(): jnp.sum(merged_down * merged_down, axis=2).astype(jnp.bfloat16)  24.2 us
    reshape x1, local copies, waits for them, and re-layouts, body(): jnp.concatenate(lax.all_to_all(jnp.stack(jnp.split(narrow_down, lax.axis_...  17.9 us
  transfers between devices with their start and end apart: 1, of which 0 were waited for; matrix products, arithmetic and copies ran while one was open for 0% of the time, Pallas kernels for 0%

profile of v2, /device:TPU:0, one launch (start us, length us, event | category | flops | bytes accessed | tf_op | source)
XLA Modules:
  0.0 738.6 jit_solution(8709787585122454427)
XLA Ops:
  0.6 24.2 %multiply_reduce_fusion = bf16[4,6400]{1,0:T(4,128)(2,1)S(1)} fusion(f32[4,6400,512]{2,1,0:T(8,128)} %param.4, bf16[4,6400,512]{2,1,0:T(8,128)(2,1)} %param.5), kind=kLoop, calls=%fused_computation.1 | loop fusion | flops 52403200 | bytes 78694400 | tf_op jit(solution)/shard_map/reduce_sum | solution.py:10
  24.9 39.3 %psum.7 = bf16[4,6400]{1,0:T(4,128)(2,1)S(1)} all-reduce(bf16[4,6400]{1,0:T(4,128)(2,1)S(1)} %multiply_reduce_fusion), channel_id=1, replica_groups=mesh['expert'=4,'shard'=8] {'shard'}, use_global_device_ids=true, to_apply=%region_1.0 | all-reduce | flops 25600 | bytes 102400 | tf_op jit(solution)/shard_map/psum | solution.py:9
  64.2 0.1 convert_sqrt_fusion
  64.3 34.3 %divide_convert_fusion = bf16[4,6400,512]{2,1,0:T(8,128)(2,1)} fusion(f32[4,6400,512]{2,1,0:T(8,128)} %param.4, bf16[4,6400,512]{2,1,0:T(8,128)(2,1)} %param.5, f32[4,6400]{1,0:T(4,128)S(1)} %convert_sqrt_fusion), kind=kLoop, calls=%fused_computation | loop fusion | flops 52428800 | bytes 104960000 | tf_op jit(solution)/shard_map/convert_element_type | solution.py:13
  98.5 3.8 fusion.7
  102.4 3.8 fusion.6
  106.2 3.8 fusion.5
  110.0 3.8 fusion.4
  113.8 3.9 fusion.3
  117.7 3.8 fusion.2
  121.5 3.8 fusion.1
  125.3 3.8 fusion
  129.1 0.0 copy-start
  129.1 0.0 copy-start.1
  129.1 6.6 all-to-all-start
  135.8 0.0 copy-done
  135.8 0.0 copy-done.1
  135.8 578.1 %all_gather.6 = bf16[4096,4]{0,1:T(4,128)(2,1)S(1)} all-gather(bf16[512,4]{0,1:T(4,128)(2,1)S(1)} %multiply_convert_fusion), channel_id=1, replica_groups=mesh['expert'=4,'shard'=8] {'shard'}, dimensions={0}, use_global_device_ids=true | all-gather | bytes 36864 | tf_op jit(solution)/shard_map/all_gather | solution.py:24
  714.0 5.4 all-gather
  719.4 0.7 reshape.17
  720.1 0.7 constant_dynamic-slice_fusion
  720.7 0.0 all-to-all-done
  720.7 17.9 %copy.9 = bf16[8,4,100,8,512]{4,3,0,2,1:T(8,128)(2,1)} copy(bf16[8,4,100,8,512]{4,3,2,1,0:T(8,128)(2,1)} %bitcast.13) | data formatting | bytes 52428800 | tf_op jit(solution)/shard_map/reshape | solution.py:14
  (1 shorter events, 0.0 us)
Async XLA Ops:
  129.1 6.6 copy-start
  129.1 6.7 copy-start.1
  129.1 591.6 %all-to-all-start = ((bf16[8,4,800,512]{3,2,1,0:T(8,128)(2,1)}), bf16[8,4,800,512]{3,2,1,0:T(8,128)(2,1)}, u32[]{:S(2)}, u32[]{:S(2)}) async-start(bf16[8,4,800,512]{3,2,1,0:T(8,128)(2,1)} %fusion), calls=%async_computation | async-start | bytes 52428800 | tf_op jit(solution)/shard_map/all_to_all | solution.py:15
